TPU v7x, 32 devices: a whole 2x2x4 slice. The times are simulated.
32 devices in a mesh: seq: 16 (over z, y, core), head: 2 (over x).
Axes of the slice: x: 2, y: 2, z: 4, core: 2. Of those that a mesh axis runs over, the one named last changes fastest.
Arguments:
- teacher: bfloat16 [1, 4096, 4096], P(None, 'seq', 'head'), may hold values from -32 to 32
- student: bfloat16 [1, 4096, 1792], P(None, 'seq', 'head'), may hold values from -32 to 32
- weights: float32 [4096], P('seq'), may hold values from 1 to 32
Outputs:
- mean_loss: float32 [], replicated
- student_grad: float32 [1, 4096, 1792], P(None, 'seq', 'head')
All inputs are finite; a program needn't handle non-finite values.
Results may differ from a plain program's by a relative error of at most 0.0011.
Values may be sent and summed in bfloat16 or wider, within the bound.
A program may use at most 128 MiB of HBM per device.

v0:
```python
import functools
import math

import jax
import jax.numpy as jnp
from jax import lax
from jax.experimental import pallas as pl
from jax.experimental.pallas import tpu as pltpu
from jax.sharding import PartitionSpec as P

TW = 256
SW = 112
LANES = 128
LOG2E = math.log2(math.e)
LN2 = math.log(2.0)
NT = (((1,), (1,)), ((), ()))


def dot_nt(a, b):
    return lax.dot_general(a, b, NT, preferred_element_type=jnp.float32)


def kernel(
    heads, group, head_shards, t_in, s_in, w_in, grad_out, loss_out,
    u_in, w_tile, t_all, u_all, w_all, state, norms, grads, landed, losses, sums,
    t_send, u_send, w_send, t_fwd, u_fwd, t_recv, u_recv, w_recv, n_send, n_recv, g_send, g_recv,
    l_send, l_recv, s_send, s_recv,
):
    n = heads * group
    block = t_in.shape[0]
    me = lax.axis_index("seq")
    shard = lax.axis_index("head")
    head = lax.div(me, group)
    member = lax.rem(me, group)
    unroll = math.gcd(n, 8)
    pair = math.gcd(heads, 2)
    t_scale = LOG2E / math.sqrt(TW)
    u_scale = LOG2E / math.sqrt(SW)

    def other_head(i):
        return lax.rem(head + i, heads)

    def source_head(i):
        return lax.rem(head + heads - i, heads)

    def other_member(i):
        return lax.rem(member + i, group)

    def remote(src, dst, send, recv, device):
        target = device if isinstance(device, dict) else {"seq": device}
        return pltpu.make_async_remote_copy(
            src_ref=src, dst_ref=dst, send_sem=send, recv_sem=recv,
            device_id=target, device_id_type=pl.DeviceIdType.MESH,
        )

    def rows(slot):
        return pl.ds(pl.multiple_of(slot * block, block), block)

    def columns(h):
        return pl.ds(pl.multiple_of(h * TW, TW), TW)

    barrier = pltpu.get_barrier_semaphore()
    for i in range(1, n):
        pl.semaphore_signal(barrier, inc=1, device_id={"seq": lax.rem(me + i, n)}, device_id_type=pl.DeviceIdType.MESH)
    for i in range(1, head_shards):
        pl.semaphore_signal(barrier, inc=1, device_id={"head": lax.rem(shard + i, head_shards)}, device_id_type=pl.DeviceIdType.MESH)
    for h in range(heads):
        u_in[h] = jnp.concatenate(
            [s_in[:, h * SW:(h + 1) * SW], jnp.zeros((block, LANES - SW), jnp.bfloat16)], axis=1
        )
    w_tile[...] = jnp.broadcast_to(w_in[...], w_tile.shape)
    pl.semaphore_wait(barrier, n + head_shards - 2)

    direct = []
    for i in range(1, heads):
        h = other_head(i)
        device = h * group + member
        direct += [
            remote(t_in.at[:, columns(h)], t_all.at[rows(me)], t_send.at[i], t_recv.at[me], device),
            remote(u_in.at[h], u_all.at[rows(me)], u_send.at[i], u_recv.at[me], device),
            remote(w_tile, w_all.at[head], w_send.at[i], w_recv.at[head], device),
        ]
    for copy in direct:
        copy.start()

    def forwards(i, slot, t_src, u_src):
        pairs = []
        for g in range(1, group):
            device = head * group + other_member(g)
            pairs += [
                remote(t_src, t_all.at[rows(slot)], t_fwd.at[i, g], t_recv.at[slot], device),
                remote(u_src, u_all.at[rows(slot)], u_fwd.at[i, g], u_recv.at[slot], device),
            ]
        return pairs

    def arrived(slot):
        remote(t_in.at[:, columns(0)], t_all.at[rows(slot)], t_send.at[0], t_recv.at[slot], me).wait_recv()
        remote(u_in.at[0], u_all.at[rows(slot)], u_send.at[0], u_recv.at[slot], me).wait_recv()

    for copy in forwards(0, me, t_in.at[:, columns(head)], u_in.at[head]):
        copy.start()
    t_all[rows(me), :] = t_in[:, columns(head)]
    u_all[rows(me), :] = u_in[head]
    w_all[head] = w_tile[...]

    low = jnp.full((8, block), -1e30, jnp.float32)
    zero = jnp.zeros((8, block), jnp.float32)
    for h in range(heads):
        for k, value in enumerate((low, zero, zero, low, zero)):
            state[h, k] = value

    def tile(row_head, key_pair):
        t_own = t_all[rows(row_head * group + member), :]
        u_own = u_all[rows(row_head * group + member), :]
        width = math.gcd(group, 2)
        parts = [(a, q) for a in range(pair) for q in range(width)]

        def step(j, carry):
            t_max, t_sum, t_cross, u_max, u_sum = carry
            for a, q in parts:
                keys = rows(source_head(key_pair * pair + a) * group + j * width + q)
                t_score = (dot_nt(t_all[keys, :], t_own) * t_scale).reshape(block // 8, 8, block)
                u_score = (dot_nt(u_all[keys, :], u_own) * u_scale).reshape(block // 8, 8, block)
                t_top = jnp.maximum(t_max, jnp.max(t_score, axis=0))
                u_top = jnp.maximum(u_max, jnp.max(u_score, axis=0))
                t_exp = jnp.exp2(t_score - t_top[None])
                u_exp = jnp.exp2(u_score - u_top[None])
                t_keep = jnp.exp2(t_max - t_top)
                u_keep = jnp.exp2(u_max - u_top)
                t_sum = t_sum * t_keep + jnp.sum(t_exp, axis=0)
                t_cross = t_cross * t_keep + jnp.sum(t_exp * (t_score - u_score), axis=0)
                u_sum = u_sum * u_keep + jnp.sum(u_exp, axis=0)
                t_max, u_max = t_top, u_top
            return t_max, t_sum, t_cross, u_max, u_sum

        carry = tuple(state[row_head, k] for k in range(5))
        carry = step(0, carry) if group == width else lax.fori_loop(0, group // width, step, carry)
        for k in range(5):
            state[row_head, k] = carry[k]

    def arrival(p, carry):
        for a in range(pair):
            i = p * pair + a
            h = source_head(i)
            slot = h * group + member

            @pl.when(i > 0)
            def _(i=i, slot=slot):
                arrived(slot)
                for copy in forwards(i, slot, t_all.at[rows(slot)], u_all.at[rows(slot)]):
                    copy.start()
        for a in range(pair):
            h = source_head(p * pair + a)
            for g in range(1, group):
                arrived(h * group + other_member(g))

        def one(j, carry):
            old = j < p * pair
            fresh = j - p * pair
            tile(
                source_head(jnp.where(old, j, p * pair + lax.rem(fresh, pair))),
                jnp.where(old, p, lax.div(fresh, pair)),
            )
            return carry

        return lax.fori_loop(0, p * pair + (p + 1) * pair, one, carry)

    lax.fori_loop(0, heads // pair, arrival, 0)
    for i in range(1, heads):
        remote(w_tile, w_all.at[source_head(i)], w_send.at[0], w_recv.at[source_head(i)], me).wait_recv()

    loss = jnp.zeros((1, block), jnp.float32)
    for i in range(heads):
        t_max, t_sum, t_cross, u_max, u_sum = (state[i, k] for k in range(5))
        t_top = jnp.max(t_max, axis=0, keepdims=True)
        u_top = jnp.max(u_max, axis=0, keepdims=True)
        t_keep = jnp.exp2(t_max - t_top)
        t_total = jnp.sum(t_sum * t_keep, axis=0, keepdims=True)
        t_mixed = jnp.sum(t_cross * t_keep, axis=0, keepdims=True)
        u_total = jnp.sum(u_sum * jnp.exp2(u_max - u_top), axis=0, keepdims=True)
        t_norm = t_top + jnp.log(t_total) * LOG2E
        u_norm = u_top + jnp.log(u_total) * LOG2E
        weight = w_all[i][:1, :]
        weight_log = jnp.log(weight) * LOG2E
        norms[member, i, 0:8, :] = jnp.broadcast_to(t_norm - weight_log, (8, block))
        norms[member, i, 8:16, :] = jnp.broadcast_to(u_norm - weight_log, (8, block))
        loss = loss + weight * (t_mixed / t_total - t_norm + u_norm)
    loss = jnp.sum(loss, axis=1, keepdims=True) * (LN2 / (heads * head_shards * block * n))
    losses[me] = jnp.broadcast_to(loss, losses.shape[1:])
    stats = [
        remote(norms.at[member], norms.at[member], n_send.at[g], n_recv.at[member], head * group + other_member(g))
        for g in range(1, group)
    ]
    for i in range(1, n):
        stats.append(remote(losses.at[me], losses.at[me], l_send.at[i], l_recv.at[me], lax.rem(me + i, n)))
    for copy in stats:
        copy.start()
    for g in range(1, group):
        m = other_member(g)
        remote(norms.at[m], norms.at[m], n_send.at[0], n_recv.at[m], me).wait_recv()

    def row_grad(i):
        slot = i * group + member
        t_own = t_all[rows(slot), :]
        u_own = u_all[rows(slot), :]

        def own_norm(first):
            tall = jnp.broadcast_to(norms[member, i, first:first + 1, :], (LANES, block)).T
            return jnp.concatenate([tall] * (block // LANES), axis=1)

        t_mine = own_norm(0)
        u_mine = own_norm(8)

        def step(j, total):
            for q in range(unroll):
                key = j * unroll + q
                keys = rows(key)
                key_head = lax.div(key, group)
                key_member = lax.rem(key, group)
                t_theirs = norms[key_member, key_head, 0:1, :]
                u_theirs = norms[key_member, key_head, 8:9, :]
                u_keys = u_all[keys, :]
                t_score = dot_nt(t_own, t_all[keys, :]) * t_scale
                u_score = dot_nt(u_own, u_keys) * u_scale
                row_part = jnp.exp2(u_score - u_mine) - jnp.exp2(t_score - t_mine)
                col_part = jnp.exp2(u_score - u_theirs) - jnp.exp2(t_score - t_theirs)
                mix = (row_part + col_part).astype(jnp.bfloat16)
                total = total + jnp.dot(mix, u_keys, preferred_element_type=jnp.float32)
            return total

        total = lax.fori_loop(0, n // unroll, step, jnp.zeros((block, LANES), jnp.float32))
        return total * (1.0 / math.sqrt(SW))

    def send_grad(i, h):
        return remote(grads.at[h], landed.at[head], g_send.at[h], g_recv.at[head], h * group + member)

    def grad_step(i, carry):
        h = other_head(i)
        grads[h] = row_grad(h)
        send_grad(i, h).start()
        return carry

    lax.fori_loop(1, heads, grad_step, 0)
    for i in range(1, n):
        peer = lax.rem(me + i, n)
        remote(losses.at[peer], losses.at[peer], l_send.at[0], l_recv.at[peer], me).wait_recv()
    sums[shard] = jnp.sum(losses[...], axis=0)
    shards = [
        remote(sums.at[shard], sums.at[shard], s_send.at[i], s_recv.at[shard], {"head": lax.rem(shard + i, head_shards)})
        for i in range(1, head_shards)
    ]
    for copy in shards:
        copy.start()
    landed[head] = row_grad(head)
    for i in range(1, head_shards):
        peer = lax.rem(shard + i, head_shards)
        remote(sums.at[peer], sums.at[peer], s_send.at[0], s_recv.at[peer], {"head": peer}).wait_recv()
    loss_out[...] = jnp.sum(sums[...], axis=0)

    for copy in direct + stats + shards:
        copy.wait_send()
    for i in range(heads):
        for copy in forwards(i, me, t_in.at[:, columns(0)], u_in.at[0]):
            copy.wait_send()
    for i in range(1, heads):
        send_grad(i, other_head(i)).wait_send()
    for h in range(heads):
        @pl.when(head != h)
        def _(h=h):
            remote(grads.at[h], landed.at[h], g_send.at[h], g_recv.at[h], me).wait_recv()
        grad_out[:, h * SW:(h + 1) * SW] = landed[h][:, :SW]


def local(teacher, student, weights):
    relations, block, t_columns = teacher.shape
    assert relations == 1
    heads = t_columns // TW
    n = lax.axis_size("seq")
    head_shards = lax.axis_size("head")
    assert n % heads == 0
    group = n // heads
    vmem = pl.BlockSpec(memory_space=pltpu.VMEM)
    dma = pltpu.SemaphoreType.DMA
    student_grad, loss = pl.pallas_call(
        functools.partial(kernel, heads, group, head_shards),
        out_shape=(
            jax.ShapeDtypeStruct((block, heads * SW), jnp.float32),
            jax.ShapeDtypeStruct((8, LANES), jnp.float32),
        ),
        in_specs=[vmem] * 3,
        out_specs=(vmem, vmem),
        scratch_shapes=[
            pltpu.VMEM((heads, block, LANES), jnp.bfloat16),
            pltpu.VMEM((8, block), jnp.float32),
            pltpu.VMEM((n * block, TW), jnp.bfloat16),
            pltpu.VMEM((n * block, LANES), jnp.bfloat16),
            pltpu.VMEM((heads, 8, block), jnp.float32),
            pltpu.VMEM((heads, 5, 8, block), jnp.float32),
            pltpu.VMEM((group, heads, 16, block), jnp.float32),
            pltpu.VMEM((heads, block, LANES), jnp.float32),
            pltpu.VMEM((heads, block, LANES), jnp.float32),
            pltpu.VMEM((n, 8, LANES), jnp.float32),
            pltpu.VMEM((head_shards, 8, LANES), jnp.float32),
            dma((heads,)), dma((heads,)), dma((heads,)),
            dma((heads, group)), dma((heads, group)),
            dma((n,)), dma((n,)), dma((heads,)),
            dma((group,)), dma((group,)),
            dma((heads,)), dma((heads,)),
            dma((n,)), dma((n,)), dma((head_shards,)), dma((head_shards,)),
        ],
        compiler_params=pltpu.CompilerParams(
            collective_id=0, has_side_effects=True, vmem_limit_bytes=60 * 2**20
        ),
    )(teacher[0], student[0], weights[None, :])
    return (loss[0, 0], student_grad[None])


def solution(mesh):
    return jax.shard_map(
        local,
        mesh=mesh,
        in_specs=(P(None, "seq", "head"), P(None, "seq", "head"), P("seq")),
        out_specs=(P(), P(None, "seq", "head")),
        check_vma=False,
    )
```

profile of v0, /device:TPU:24, one launch (start us, length us, event | category | flops | bytes accessed | tf_op | source)
XLA Modules:
  0.0 110.9 jit_solution(1350009425957316727)
XLA Ops:
  0.6 107.0 %shard_map.50 = (f32[256,896]{1,0:T(8,128)}, f32[8,128]{1,0:T(8,128)}) custom-call(bf16[256,2048]{1,0:T(8,128)(2,1)} %bitcast.5, bf16[256,896]{1,0:T(8,128)(2,1)} %bitcast.7, f32[1,256]{1,0:T(1,128)} %bitcast.8), custom_call_target="tpu_custom_call" | custom-call | tf_op jit(solution)/shard_map/pallas_call | solution.py:284
  107.6 1.2 %slice.3 = f32[1,1]{1,0:T(1,128)} slice(f32[8,128]{1,0:T(8,128)} %get-tuple-element.4), slice={[0:1], [0:1]} | slice | bytes 8 | tf_op jit(solution)/shard_map/slice | solution.py:315
  108.8 2.2 %copy.6 = f32[1,256,896]{2,1,0:T(8,128)} copy(f32[1,256,896]{2,1,0:T(8,128)} %bitcast.6) | data formatting | bytes 1835008
where the time goes:
time: 111 us
  Pallas kernels  107 us (96%)
  local copies, waits for them, and re-layouts  3.35 us (3%)
    pallas_call x1, Pallas kernels, local(): pl.pallas_call(functools.partial(kernel, heads, group, head_shards), out_...  107 us

commit v1 on v0

--- a/solution.py
+++ b/solution.py
@@ -11,6 +11,7 @@
 TW = 256
 SW = 112
 LANES = 128
+SPAN = 119.0
 LOG2E = math.log2(math.e)
 LN2 = math.log(2.0)
 NT = (((1,), (1,)), ((), ()))
@@ -271,6 +272,328 @@
         grad_out[:, h * SW:(h + 1) * SW] = landed[h][:, :SW]
 
 
+def pair_kernel(
+    heads, head_shards, t_in, s_in, w_in, grad_out, loss_out,
+    u_in, w_tile, t_all, u_all, u_turn, w_all, t_raw, u_raw, t_exp, u_exp, t_refs, u_refs, t_top, u_top, cross,
+    t_rows, u_rows, parts, landed_parts, grads, code_out, code_in, landed, losses, sums,
+    t_send, u_send, w_send, t_fwd, u_fwd, t_recv, u_recv, w_recv, p_send, p_recv, g_send, g_recv,
+    l_send, l_recv, s_send, s_recv,
+):
+    group = 2
+    n = heads * group
+    block = t_in.shape[0]
+    both = group * block
+    me = lax.axis_index("seq")
+    shard = lax.axis_index("head")
+    head = lax.div(me, group)
+    member = lax.rem(me, group)
+    mate = head * group + 1 - member
+    bits = (heads - 1).bit_length()
+    t_scale = LOG2E / math.sqrt(TW)
+    u_scale = LOG2E / math.sqrt(SW)
+
+    def flip(i):
+        out = 0
+        for k in range(bits):
+            out = out + lax.rem(lax.div(head, 2**k) + lax.div(jnp.int32(i), 2**k), 2) * 2**k
+        return out
+
+    def remote(src, dst, send, recv, device):
+        target = device if isinstance(device, dict) else {"seq": device}
+        return pltpu.make_async_remote_copy(
+            src_ref=src, dst_ref=dst, send_sem=send, recv_sem=recv,
+            device_id=target, device_id_type=pl.DeviceIdType.MESH,
+        )
+
+    def rows(slot):
+        return pl.ds(pl.multiple_of(slot * block, block), block)
+
+    def both_rows(h):
+        return pl.ds(pl.multiple_of(h * both, both), both)
+
+    def head_rows(h):
+        return pl.ds(pl.multiple_of(h * SW, 16), SW)
+
+    def columns(h):
+        return pl.ds(pl.multiple_of(h * TW, TW), TW)
+
+    barrier = pltpu.get_barrier_semaphore()
+    for i in range(1, n):
+        pl.semaphore_signal(barrier, inc=1, device_id={"seq": lax.rem(me + i, n)}, device_id_type=pl.DeviceIdType.MESH)
+    for i in range(1, head_shards):
+        pl.semaphore_signal(barrier, inc=1, device_id={"head": lax.rem(shard + i, head_shards)}, device_id_type=pl.DeviceIdType.MESH)
+    for c in range(heads * SW // LANES):
+        piece = s_in[:, c * LANES:(c + 1) * LANES].astype(jnp.float32)
+        u_in[c * LANES:(c + 1) * LANES, :] = piece.T.astype(jnp.bfloat16)
+    spare = lax.broadcasted_iota(jnp.int32, (LANES - SW, block), 0)
+    ones = jnp.where(spare == 0, 1.0, 0.0).astype(jnp.bfloat16)
+    for k in range(n):
+        u_turn[k, SW:, :] = ones
+    w_tile[...] = jnp.broadcast_to(w_in[...], w_tile.shape)
+    pl.semaphore_wait(barrier, n + head_shards - 2)
+
+    direct = []
+    for i in range(1, heads):
+        h = flip(i)
+        device = h * group + member
+        direct += [
+            remote(t_in.at[:, columns(h)], t_all.at[rows(me)], t_send.at[i], t_recv.at[me], device),
+            remote(u_in.at[head_rows(h)], u_turn.at[me, pl.ds(0, SW)], u_send.at[i], u_recv.at[me], device),
+            remote(w_tile, w_all.at[head], w_send.at[i], w_recv.at[head], device),
+        ]
+    for copy in direct:
+        copy.start()
+
+    def forwards(i, slot, t_src, u_src):
+        return [
+            remote(t_src, t_all.at[rows(slot)], t_fwd.at[i], t_recv.at[slot], mate),
+            remote(u_src, u_turn.at[slot, pl.ds(0, SW)], u_fwd.at[i], u_recv.at[slot], mate),
+        ]
+
+    def arrived(slot):
+        remote(t_in.at[:, columns(0)], t_all.at[rows(slot)], t_send.at[0], t_recv.at[slot], mate).wait_recv()
+        remote(u_in.at[head_rows(0)], u_turn.at[slot, pl.ds(0, SW)], u_send.at[0], u_recv.at[slot], mate).wait_recv()
+
+    for copy in forwards(0, me, t_in.at[:, columns(head)], u_in.at[head_rows(head)]):
+        copy.start()
+    t_all[rows(me), :] = t_in[:, columns(head)]
+    u_turn[me, :SW, :] = u_in[head_rows(head), :]
+    w_all[head] = w_tile[...]
+    lane = lax.broadcasted_iota(jnp.int32, (block, LANES), 1)
+
+    def turn_u(slot):
+        u_all[rows(slot), :] = jnp.where(lane < SW, u_turn[slot].astype(jnp.float32).T, 0.0).astype(jnp.bfloat16)
+
+    for h in range(heads):
+        t_top[h] = jnp.full((8, block), -1e30, jnp.float32)
+        u_top[h] = jnp.full((8, block), -1e30, jnp.float32)
+        cross[h] = jnp.zeros((8, block), jnp.float32)
+        t_rows[h] = jnp.zeros((LANES, block), jnp.float32)
+        u_rows[h] = jnp.zeros((LANES, block), jnp.float32)
+
+    def fold(x, op):
+        return op(x.reshape(x.shape[0] // 8, 8, block), axis=0)
+
+    def unit(i, k):
+        early = k < i
+        return flip(jnp.where(early, i, k - i)), flip(jnp.where(early, k, i))
+
+    def scores(i, k, b):
+        own, key = unit(i, k)
+        slot = own * group + member
+        t = dot_nt(t_all[both_rows(key), :], t_all[rows(slot), :])
+        u = jnp.dot(u_all[both_rows(key), :], u_turn[slot], preferred_element_type=jnp.float32)
+        t_raw[b] = t
+        u_raw[b] = u
+        return fold(t, jnp.max), fold(u, jnp.max)
+
+    def soften(i, k, b, peaks):
+        own, key = unit(i, k)
+
+        def side(raw_ref, peak, scale, top, refs, exps, out, with_cross):
+            raw = raw_ref[b]
+            old = top[own]
+            new = jnp.maximum(old, jnp.max(peak, axis=0, keepdims=True))
+            top[own] = new
+            refs[own, pl.ds(key, 1), :] = new[:1] * scale
+            value = jnp.exp2(raw * scale - new[:1] * scale).astype(jnp.bfloat16)
+            keep = jnp.exp2((old - new) * scale)
+            if with_cross:
+                cross[own] = cross[own] * keep + fold(value.astype(jnp.float32) * raw, jnp.sum)
+            total = out[own] * keep[:1]
+            for q in range(group):
+                piece = value[q * block:(q + 1) * block]
+                exps[own, key * group + q] = piece
+                total = total + jnp.dot(u_turn[key * group + q], piece, preferred_element_type=jnp.float32)
+            out[own] = total
+
+        side(t_raw, peaks[0], t_scale, t_top, t_refs, t_exp, t_rows, True)
+        side(u_raw, peaks[1], u_scale, u_top, u_refs, u_exp, u_rows, False)
+
+    turn_u(me)
+    arrived(head * group + 1 - member)
+    turn_u(head * group + 1 - member)
+    soften(0, 0, 0, scores(0, 0, 0))
+
+    def arrival(i, carry):
+        h = flip(i)
+        slot = h * group + member
+        other = h * group + 1 - member
+        arrived(slot)
+        for copy in forwards(i, slot, t_all.at[rows(slot)], u_turn.at[slot, pl.ds(0, SW)]):
+            copy.start()
+        turn_u(slot)
+
+        def two(j, peaks):
+            @pl.when(j == lax.div(i - 1, 2))
+            def _():
+                arrived(other)
+                turn_u(other)
+            k = 2 * j
+            later = scores(i, k + 1, 1)
+            soften(i, k, 0, peaks)
+            peaks = scores(i, k + 2, 0)
+            soften(i, k + 1, 1, later)
+            return peaks
+
+        soften(i, 2 * i, 0, lax.fori_loop(0, i, two, scores(i, 0, 0)))
+        return carry
+
+    lax.fori_loop(1, heads, arrival, 0)
+    for i in range(1, heads):
+        remote(w_tile, w_all.at[flip(i)], w_send.at[0], w_recv.at[flip(i)], mate).wait_recv()
+
+    loss = jnp.zeros((1, block), jnp.float32)
+    for h in range(heads):
+        weight = w_all[h][:1, :]
+        t_sum = t_rows[h, SW:SW + 1, :]
+        u_sum = u_rows[h, SW:SW + 1, :]
+        t_norm = t_top[h][:1] * t_scale + jnp.log(t_sum) * LOG2E
+        u_norm = u_top[h][:1] * u_scale + jnp.log(u_sum) * LOG2E
+        own_u = u_turn[h * group + member].astype(jnp.float32)[:SW]
+        seen = jnp.sum(own_u * t_rows[h, :SW, :], axis=0, keepdims=True) * u_scale
+        mean = (jnp.sum(cross[h], axis=0, keepdims=True) * t_scale - seen) / t_sum
+        loss = loss + weight * (mean - t_norm + u_norm)
+        t_part = weight / t_sum
+        u_part = weight / u_sum
+        t_last = t_top[h][:1] * t_scale
+        u_last = u_top[h][:1] * u_scale
+        t_refs[h] = jnp.exp2(t_refs[h] - t_last) * t_part
+        u_refs[h] = jnp.exp2(u_refs[h] - u_last) * u_part
+        u_rows[h] = u_rows[h] * u_part - t_rows[h] * t_part
+    loss = jnp.sum(loss, axis=1, keepdims=True) * (LN2 / (heads * head_shards * block * n))
+    losses[me] = jnp.broadcast_to(loss, losses.shape[1:])
+    stats = [
+        remote(losses.at[me], losses.at[me], l_send.at[i], l_recv.at[me], lax.rem(me + i, n))
+        for i in range(1, n)
+    ]
+    for copy in stats:
+        copy.start()
+
+    def column_part(h, q):
+        key = h * group + q
+        total = jnp.zeros((LANES, block), jnp.float32)
+        for own in range(heads):
+            t_part = t_exp[own, key].astype(jnp.float32) * t_refs[own, pl.ds(h, 1), :]
+            u_part = u_exp[own, key].astype(jnp.float32) * u_refs[own, pl.ds(h, 1), :]
+            total = total + dot_nt(u_turn[own * group + member], (u_part - t_part).astype(jnp.bfloat16))
+        return total[:SW]
+
+    def swap(h):
+        return remote(parts.at[h], landed_parts.at[h], p_send.at[h], p_recv.at[h], mate)
+
+    def give(i, h):
+        return remote(code_out.at[h], code_in.at[head], g_send.at[i], g_recv.at[head], h * group + member)
+
+    def finish(h):
+        swap(h).wait_recv()
+        return (grads[h] + landed_parts[h]) * (1.0 / math.sqrt(SW))
+
+    def hand_over(i):
+        h = flip(i)
+        grad = finish(h)
+        peak = jnp.maximum(jnp.max(jnp.abs(grad), axis=0, keepdims=True), 1e-30)
+        peak = (peak * 1.01).astype(jnp.bfloat16)
+        code_out[h, SW:, :] = jnp.broadcast_to(peak, (LANES - SW, block))
+        code_out[h, :SW, :] = jnp.exp2(grad * (SPAN / peak.astype(jnp.float32))).astype(jnp.bfloat16)
+        give(i, h).start()
+
+    def step(j, carry):
+        i = heads - 1 - j
+        h = flip(i)
+        parts[h] = column_part(h, 1 - member)
+        swap(h).start()
+
+        @pl.when(j > 0)
+        def _():
+            hand_over(i + 1)
+        grads[h] = column_part(h, member) + u_rows[h, :SW, :]
+        return carry
+
+    lax.fori_loop(0, heads, step, 0)
+    for i in range(1, n):
+        peer = lax.rem(me + i, n)
+        remote(losses.at[peer], losses.at[peer], l_send.at[0], l_recv.at[peer], mate).wait_recv()
+    sums[shard] = jnp.sum(losses[...], axis=0)
+    shards = [
+        remote(sums.at[shard], sums.at[shard], s_send.at[i], s_recv.at[shard], {"head": lax.rem(shard + i, head_shards)})
+        for i in range(1, head_shards)
+    ]
+    for copy in shards:
+        copy.start()
+    landed[head_rows(head), :] = finish(head)
+    for i in range(1, head_shards):
+        peer = lax.rem(shard + i, head_shards)
+        remote(sums.at[peer], sums.at[peer], s_send.at[0], s_recv.at[peer], {"head": peer}).wait_recv()
+    loss_out[...] = jnp.sum(sums[...], axis=0)
+
+    for copy in direct + stats + shards:
+        copy.wait_send()
+    for i in range(heads):
+        for copy in forwards(i, me, t_in.at[:, columns(0)], u_in.at[head_rows(0)]):
+            copy.wait_send()
+        swap(flip(i)).wait_send()
+    for i in range(1, heads):
+        give(i, flip(i)).wait_send()
+    for i in range(1, heads):
+        h = flip(i)
+        remote(code_out.at[h], code_in.at[h], g_send.at[0], g_recv.at[h], mate).wait_recv()
+        code = code_in[h].astype(jnp.float32)
+        landed[head_rows(h), :] = jnp.log(code[:SW]) * (code[SW:SW + 1] * (LOG2E / SPAN))
+    for c in range(heads * SW // LANES):
+        grad_out[:, c * LANES:(c + 1) * LANES] = landed[c * LANES:(c + 1) * LANES, :].T
+
+def pair_call(heads, n, head_shards, block):
+    vmem = pl.BlockSpec(memory_space=pltpu.VMEM)
+    dma = pltpu.SemaphoreType.DMA
+    f32, bf16 = jnp.float32, jnp.bfloat16
+    return pl.pallas_call(
+        functools.partial(pair_kernel, heads, head_shards),
+        out_shape=(
+            jax.ShapeDtypeStruct((block, heads * SW), f32),
+            jax.ShapeDtypeStruct((8, LANES), f32),
+        ),
+        in_specs=[vmem] * 3,
+        out_specs=(vmem, vmem),
+        scratch_shapes=[
+            pltpu.VMEM((heads * SW, block), bf16),
+            pltpu.VMEM((8, block), f32),
+            pltpu.VMEM((n * block, TW), bf16),
+            pltpu.VMEM((n * block, LANES), bf16),
+            pltpu.VMEM((n, LANES, block), bf16),
+            pltpu.VMEM((heads, 8, block), f32),
+            pltpu.VMEM((2, 2 * block, block), f32),
+            pltpu.VMEM((2, 2 * block, block), f32),
+            pltpu.VMEM((heads, n, block, block), bf16),
+            pltpu.VMEM((heads, n, block, block), bf16),
+            pltpu.VMEM((heads, heads, block), f32),
+            pltpu.VMEM((heads, heads, block), f32),
+            pltpu.VMEM((heads, 8, block), f32),
+            pltpu.VMEM((heads, 8, block), f32),
+            pltpu.VMEM((heads, 8, block), f32),
+            pltpu.VMEM((heads, LANES, block), f32),
+            pltpu.VMEM((heads, LANES, block), f32),
+            pltpu.VMEM((heads, SW, block), f32),
+            pltpu.VMEM((heads, SW, block), f32),
+            pltpu.VMEM((heads, SW, block), f32),
+            pltpu.VMEM((heads, LANES, block), bf16),
+            pltpu.VMEM((heads, LANES, block), bf16),
+            pltpu.VMEM((heads * SW, block), f32),
+            pltpu.VMEM((n, 8, LANES), f32),
+            pltpu.VMEM((head_shards, 8, LANES), f32),
+            dma((heads,)), dma((heads,)), dma((heads,)),
+            dma((heads,)), dma((heads,)),
+            dma((n,)), dma((n,)), dma((heads,)),
+            dma((heads,)), dma((heads,)),
+            dma((heads,)), dma((heads,)),
+            dma((n,)), dma((n,)), dma((head_shards,)), dma((head_shards,)),
+        ],
+        compiler_params=pltpu.CompilerParams(
+            collective_id=1, has_side_effects=True, vmem_limit_bytes=60 * 2**20
+        ),
+    )
+
+
 def local(teacher, student, weights):
     relations, block, t_columns = teacher.shape
     assert relations == 1
@@ -279,6 +602,9 @@
     head_shards = lax.axis_size("head")
     assert n % heads == 0
     group = n // heads
+    if group == 2 and heads & (heads - 1) == 0 and heads * SW % LANES == 0 and n * n * block * block <= 2**24:
+        student_grad, loss = pair_call(heads, n, head_shards, block)(teacher[0], student[0], weights[None, :])
+        return (loss[0, 0], student_grad[None])
     vmem = pl.BlockSpec(memory_space=pltpu.VMEM)
     dma = pltpu.SemaphoreType.DMA
     student_grad, loss = pl.pallas_call(

time: 111 us -> 74.1 us (0.67)
  the two profiles are of different devices: /device:TPU:24 before, /device:TPU:0 now
where the time goes in v1:
time: 74.1 us; the launch traced here: 73.9 us
  Pallas kernels  69.9 us (94%)
  local copies, waits for them, and re-layouts  3.35 us (5%)
    pallas_call x1, Pallas kernels, local(): pair_call(heads, n, head_shards, block)  69.9 us
    unnamed x1, local copies, waits for them, and re-layouts  2.16 us

profile of v1, /device:TPU:0, one launch (start us, length us, event | category | flops | bytes accessed | tf_op | source)
XLA Modules:
  0.0 73.9 jit_solution(4144724715517291459)
XLA Ops:
  0.6 69.9 %shard_map.50 = (f32[256,896]{1,0:T(8,128)}, f32[8,128]{1,0:T(8,128)}) custom-call(bf16[256,2048]{1,0:T(8,128)(2,1)} %bitcast.5, bf16[256,896]{1,0:T(8,128)(2,1)} %bitcast.7, f32[1,256]{1,0:T(1,128)} %bitcast.8), custom_call_target="tpu_custom_call" | custom-call | tf_op jit(solution)/shard_map/pallas_call | solution.py:606
  70.6 1.2 %slice.3 = f32[1,1]{1,0:T(1,128)} slice(f32[8,128]{1,0:T(8,128)} %get-tuple-element.4), slice={[0:1], [0:1]} | slice | bytes 8 | tf_op jit(solution)/shard_map/slice | solution.py:607
  71.7 2.2 %copy.6 = f32[1,256,896]{2,1,0:T(8,128)} copy(f32[1,256,896]{2,1,0:T(8,128)} %bitcast.6) | data formatting | bytes 1835008

commit v2 on v1

--- a/solution.py
+++ b/solution.py
@@ -273,11 +273,11 @@
 
 
 def pair_kernel(
-    heads, head_shards, t_in, s_in, w_in, grad_out, loss_out,
+    heads, head_shards, t_in, s_in, w_in, code_in, loss_out,
     u_in, w_tile, t_all, u_all, u_turn, w_all, t_raw, u_raw, t_exp, u_exp, t_refs, u_refs, t_top, u_top, cross,
-    t_rows, u_rows, parts, landed_parts, grads, code_out, code_in, landed, losses, sums,
+    t_rows, u_rows, parts, landed_parts, grads, code_out, losses, sums,
     t_send, u_send, w_send, t_fwd, u_fwd, t_recv, u_recv, w_recv, p_send, p_recv, g_send, g_recv,
-    l_send, l_recv, s_send, s_recv,
+    l_send, l_recv, s_send, s_recv, own_sem,
 ):
     group = 2
     n = heads * group
@@ -356,7 +356,8 @@
 
     for copy in forwards(0, me, t_in.at[:, columns(head)], u_in.at[head_rows(head)]):
         copy.start()
-    t_all[rows(me), :] = t_in[:, columns(head)]
+    own_t = pltpu.make_async_copy(t_in.at[:, columns(head)], t_all.at[rows(me)], own_sem.at[0])
+    own_t.start()
     u_turn[me, :SW, :] = u_in[head_rows(head), :]
     w_all[head] = w_tile[...]
     lane = lax.broadcasted_iota(jnp.int32, (block, LANES), 1)
@@ -411,6 +412,7 @@
         side(u_raw, peaks[1], u_scale, u_top, u_refs, u_exp, u_rows, False)
 
     turn_u(me)
+    own_t.wait()
     arrived(head * group + 1 - member)
     turn_u(head * group + 1 - member)
     soften(0, 0, 0, scores(0, 0, 0))
@@ -424,19 +426,27 @@
             copy.start()
         turn_u(slot)
 
+        def run(k, count, peaks):
+            for z in range(count):
+                ahead = scores(i, k + z + 1, (z + 1) % 2)
+                soften(i, k + z, z % 2, peaks)
+                peaks = ahead
+            return peaks
+
+        def whole():
+            arrived(other)
+            turn_u(other)
+
+        def four(j, peaks):
+            pl.when(j == lax.div(i - 1, 4))(whole)
+            return run(4 * j, 4, peaks)
+
         def two(j, peaks):
-            @pl.when(j == lax.div(i - 1, 2))
-            def _():
-                arrived(other)
-                turn_u(other)
-            k = 2 * j
-            later = scores(i, k + 1, 1)
-            soften(i, k, 0, peaks)
-            peaks = scores(i, k + 2, 0)
-            soften(i, k + 1, 1, later)
-            return peaks
-
-        soften(i, 2 * i, 0, lax.fori_loop(0, i, two, scores(i, 0, 0)))
+            pl.when(i == 1)(whole)
+            return run(2 * i - 2, 2, peaks)
+
+        peaks = lax.fori_loop(0, lax.div(i, 2), four, scores(i, 0, 0))
+        soften(i, 2 * i, 0, lax.fori_loop(0, lax.rem(i, 2), two, peaks))
         return carry
 
     lax.fori_loop(1, heads, arrival, 0)
@@ -489,13 +499,16 @@
         swap(h).wait_recv()
         return (grads[h] + landed_parts[h]) * (1.0 / math.sqrt(SW))
 
-    def hand_over(i):
-        h = flip(i)
+    def encode(h):
         grad = finish(h)
         peak = jnp.maximum(jnp.max(jnp.abs(grad), axis=0, keepdims=True), 1e-30)
         peak = (peak * 1.01).astype(jnp.bfloat16)
         code_out[h, SW:, :] = jnp.broadcast_to(peak, (LANES - SW, block))
         code_out[h, :SW, :] = jnp.exp2(grad * (SPAN / peak.astype(jnp.float32))).astype(jnp.bfloat16)
+
+    def hand_over(i):
+        h = flip(i)
+        encode(h)
         give(i, h).start()
 
     def step(j, carry):
@@ -521,11 +534,13 @@
     ]
     for copy in shards:
         copy.start()
-    landed[head_rows(head), :] = finish(head)
+    encode(head)
+    own_code = pltpu.make_async_copy(code_out.at[head], code_in.at[head], own_sem.at[1])
+    own_code.start()
     for i in range(1, head_shards):
         peer = lax.rem(shard + i, head_shards)
         remote(sums.at[peer], sums.at[peer], s_send.at[0], s_recv.at[peer], {"head": peer}).wait_recv()
-    loss_out[...] = jnp.sum(sums[...], axis=0)
+    loss_out[0, 0] = jnp.max(jnp.sum(sums[...], axis=0))
 
     for copy in direct + stats + shards:
         copy.wait_send()
@@ -535,13 +550,48 @@
         swap(flip(i)).wait_send()
     for i in range(1, heads):
         give(i, flip(i)).wait_send()
+    own_code.wait()
     for i in range(1, heads):
         h = flip(i)
         remote(code_out.at[h], code_in.at[h], g_send.at[0], g_recv.at[h], mate).wait_recv()
-        code = code_in[h].astype(jnp.float32)
-        landed[head_rows(h), :] = jnp.log(code[:SW]) * (code[SW:SW + 1] * (LOG2E / SPAN))
-    for c in range(heads * SW // LANES):
-        grad_out[:, c * LANES:(c + 1) * LANES] = landed[c * LANES:(c + 1) * LANES, :].T
+
+def decode_kernel(heads, codes, loss_in, grad_out, loss_out, flat, tall, sem):
+    loss_out[0, 0] = loss_in[0, 0]
+    chunks = heads * SW // LANES
+
+    def write(c):
+        columns = pl.ds(c * LANES, LANES)
+        return pltpu.make_async_copy(tall.at[:, columns], grad_out.at[:, columns], sem.at[c])
+
+    ready = 0
+    for h in range(heads):
+        code = codes[h].astype(jnp.float32)
+        flat[h * SW:(h + 1) * SW, :] = jnp.log(code[:SW]) * (code[SW:SW + 1] * (LOG2E / SPAN))
+        while (ready + 1) * LANES <= (h + 1) * SW:
+            tall[:, ready * LANES:(ready + 1) * LANES] = flat[ready * LANES:(ready + 1) * LANES, :].T
+            write(ready).start()
+            ready += 1
+    for c in range(chunks):
+        write(c).wait()
+
+
+def decode_call(heads, block):
+    smem = pl.BlockSpec(memory_space=pltpu.SMEM)
+    return pl.pallas_call(
+        functools.partial(decode_kernel, heads),
+        out_shape=(
+            jax.ShapeDtypeStruct((block, heads * SW), jnp.float32),
+            jax.ShapeDtypeStruct((1, 1), jnp.float32),
+        ),
+        in_specs=[pl.BlockSpec(memory_space=pltpu.VMEM), smem],
+        out_specs=(pl.BlockSpec(memory_space=pl.ANY), smem),
+        scratch_shapes=[
+            pltpu.VMEM((heads * SW, block), jnp.float32),
+            pltpu.VMEM((block, heads * SW), jnp.float32),
+            pltpu.SemaphoreType.DMA((heads * SW // LANES,)),
+        ],
+    )
+
 
 def pair_call(heads, n, head_shards, block):
     vmem = pl.BlockSpec(memory_space=pltpu.VMEM)
@@ -550,11 +600,11 @@
     return pl.pallas_call(
         functools.partial(pair_kernel, heads, head_shards),
         out_shape=(
-            jax.ShapeDtypeStruct((block, heads * SW), f32),
-            jax.ShapeDtypeStruct((8, LANES), f32),
+            jax.ShapeDtypeStruct((heads, LANES, block), bf16),
+            jax.ShapeDtypeStruct((1, 1), f32),
         ),
-        in_specs=[vmem] * 3,
-        out_specs=(vmem, vmem),
+        in_specs=[pl.BlockSpec(memory_space=pl.ANY), vmem, vmem],
+        out_specs=(pl.BlockSpec(memory_space=pl.ANY), pl.BlockSpec(memory_space=pltpu.SMEM)),
         scratch_shapes=[
             pltpu.VMEM((heads * SW, block), bf16),
             pltpu.VMEM((8, block), f32),
@@ -577,8 +627,6 @@
             pltpu.VMEM((heads, SW, block), f32),
             pltpu.VMEM((heads, SW, block), f32),
             pltpu.VMEM((heads, LANES, block), bf16),
-            pltpu.VMEM((heads, LANES, block), bf16),
-            pltpu.VMEM((heads * SW, block), f32),
             pltpu.VMEM((n, 8, LANES), f32),
             pltpu.VMEM((head_shards, 8, LANES), f32),
             dma((heads,)), dma((heads,)), dma((heads,)),
@@ -586,7 +634,7 @@
             dma((n,)), dma((n,)), dma((heads,)),
             dma((heads,)), dma((heads,)),
             dma((heads,)), dma((heads,)),
-            dma((n,)), dma((n,)), dma((head_shards,)), dma((head_shards,)),
+            dma((n,)), dma((n,)), dma((head_shards,)), dma((head_shards,)), dma((2,)),
         ],
         compiler_params=pltpu.CompilerParams(
             collective_id=1, has_side_effects=True, vmem_limit_bytes=60 * 2**20
@@ -603,8 +651,9 @@
     assert n % heads == 0
     group = n // heads
     if group == 2 and heads & (heads - 1) == 0 and heads * SW % LANES == 0 and n * n * block * block <= 2**24:
-        student_grad, loss = pair_call(heads, n, head_shards, block)(teacher[0], student[0], weights[None, :])
-        return (loss[0, 0], student_grad[None])
+        codes, loss = pair_call(heads, n, head_shards, block)(teacher[0], student[0], weights[None, :])
+        student_grad, loss = decode_call(heads, block)(codes, loss)
+        return (loss.reshape(()), student_grad[None])
     vmem = pl.BlockSpec(memory_space=pltpu.VMEM)
     dma = pltpu.SemaphoreType.DMA
     student_grad, loss = pl.pallas_call(

time: 74.1 us -> 72 us (0.972)
  local copies, waits for them, and re-layouts: 3.35 us -> 0 us
  Pallas kernels: 69.9 us -> 71.2 us
    pallas_call x0 -> x1, Pallas kernels: none -> 3.27 us  [local(): student_grad, loss = decode_call(heads, block)(codes, loss)]
    unnamed x1 -> x0, local copies, waits for them, and re-layouts: 2.16 us -> none
    pallas_call x1, Pallas kernels: 69.9 us -> 67.9 us  [local(): pair_call(heads, n, head_shards, block)]
    slice x1 -> x0, local copies, waits for them, and re-layouts: 1.19 us -> none  [local(): return (loss[0, 0], student_grad[None])]
where the time goes in v2:
time: 72 us; the launch traced here: 71.8 us
  Pallas kernels  71.2 us (99%)
    pallas_call x1, Pallas kernels, local(): pair_call(heads, n, head_shards, block)  67.9 us
    pallas_call x1, Pallas kernels, local(): student_grad, loss = decode_call(heads, block)(codes, loss)  3.27 us

profile of v2, /device:TPU:0, one launch (start us, length us, event | category | flops | bytes accessed | tf_op | source)
XLA Modules:
  0.0 71.8 jit_solution(14602263024071458330)
XLA Ops:
  0.6 67.9 %shard_map.50 = (bf16[8,128,256]{2,1,0:T(8,128)(2,1)}, f32[1,1]{1,0:T(1,128)}) custom-call(bf16[256,2048]{1,0:T(8,128)(2,1)} %bitcast.5, bf16[256,896]{1,0:T(8,128)(2,1)} %bitcast.6, f32[1,256]{1,0:T(1,128)} %bitcast.7), custom_call_target="tpu_custom_call" | custom-call | tf_op jit(solution)/shard_map/pallas_call | solution.py:654
  68.5 3.3 %shard_map.51 = (f32[256,896]{1,0:T(8,128)}, f32[1,1]{1,0:T(1,128)}) custom-call(bf16[8,128,256]{2,1,0:T(8,128)(2,1)} %get-tuple-element.6.codes, f32[1,1]{1,0:T(1,128)} %get-tuple-element.7.loss_in), custom_call_target="tpu_custom_call" | custom-call | tf_op jit(solution)/shard_map/pallas_call | solution.py:655

commit v3 on v2

--- a/solution.py
+++ b/solution.py
@@ -273,11 +273,11 @@
 
 
 def pair_kernel(
-    heads, head_shards, t_in, s_in, w_in, code_in, loss_out,
+    heads, head_shards, t_in, s_in, w_in, code_in, peak_in, loss_out,
     u_in, w_tile, t_all, u_all, u_turn, w_all, t_raw, u_raw, t_exp, u_exp, t_refs, u_refs, t_top, u_top, cross,
-    t_rows, u_rows, parts, landed_parts, grads, code_out, losses, sums,
+    t_rows, u_rows, parts, landed_parts, code_out, peak_out, losses, sums,
     t_send, u_send, w_send, t_fwd, u_fwd, t_recv, u_recv, w_recv, p_send, p_recv, g_send, g_recv,
-    l_send, l_recv, s_send, s_recv, own_sem,
+    l_send, l_recv, s_send, s_recv, own_sem, k_send, k_recv,
 ):
     group = 2
     n = heads * group
@@ -292,7 +292,14 @@
     t_scale = LOG2E / math.sqrt(TW)
     u_scale = LOG2E / math.sqrt(SW)
 
+    half = heads // 2
+    quarter = max(heads // 4, 1)
+
     def flip(i):
+        i = jnp.int32(i)
+        if heads >= 4:
+            turned = half + lax.rem(i - half, 2) * quarter + lax.div(i - half, 2)
+            i = i + lax.div(i, half) * (turned - i)
         out = 0
         for k in range(bits):
             out = out + lax.rem(lax.div(head, 2**k) + lax.div(jnp.int32(i), 2**k), 2) * 2**k
@@ -480,47 +487,52 @@
     for copy in stats:
         copy.start()
 
-    def column_part(h, q):
-        key = h * group + q
-        total = jnp.zeros((LANES, block), jnp.float32)
+    def column_parts(h):
+        total = jnp.zeros((both, LANES), jnp.float32)
         for own in range(heads):
-            t_part = t_exp[own, key].astype(jnp.float32) * t_refs[own, pl.ds(h, 1), :]
-            u_part = u_exp[own, key].astype(jnp.float32) * u_refs[own, pl.ds(h, 1), :]
-            total = total + dot_nt(u_turn[own * group + member], (u_part - t_part).astype(jnp.bfloat16))
-        return total[:SW]
+            t_part = t_exp[own, pl.ds(h * group, group)].astype(jnp.float32) * t_refs[own, pl.ds(h, 1), :]
+            u_part = u_exp[own, pl.ds(h * group, group)].astype(jnp.float32) * u_refs[own, pl.ds(h, 1), :]
+            mix = (u_part - t_part).astype(jnp.bfloat16).reshape(both, block)
+            total = total + jnp.dot(
+                mix, u_all[rows(own * group + member), :], preferred_element_type=jnp.float32
+            )
+        for q in range(group):
+            parts[h, q] = total[q * block:(q + 1) * block].T[:SW]
 
     def swap(h):
-        return remote(parts.at[h], landed_parts.at[h], p_send.at[h], p_recv.at[h], mate)
+        return remote(parts.at[h, 1 - member], landed_parts.at[h], p_send.at[h], p_recv.at[h], mate)
 
     def give(i, h):
         return remote(code_out.at[h], code_in.at[head], g_send.at[i], g_recv.at[head], h * group + member)
 
+    def give_peak(i, h):
+        return remote(peak_out.at[h], peak_in.at[head], k_send.at[i], k_recv.at[head], h * group + member)
+
     def finish(h):
         swap(h).wait_recv()
-        return (grads[h] + landed_parts[h]) * (1.0 / math.sqrt(SW))
+        return (parts[h, member] + u_rows[h, :SW, :] + landed_parts[h]) * (1.0 / math.sqrt(SW))
 
     def encode(h):
         grad = finish(h)
         peak = jnp.maximum(jnp.max(jnp.abs(grad), axis=0, keepdims=True), 1e-30)
-        peak = (peak * 1.01).astype(jnp.bfloat16)
-        code_out[h, SW:, :] = jnp.broadcast_to(peak, (LANES - SW, block))
-        code_out[h, :SW, :] = jnp.exp2(grad * (SPAN / peak.astype(jnp.float32))).astype(jnp.bfloat16)
+        code_out[h] = jnp.exp2(grad * (SPAN / peak)).astype(jnp.bfloat16)
+        peak_out[h] = peak
 
     def hand_over(i):
         h = flip(i)
         encode(h)
         give(i, h).start()
+        give_peak(i, h).start()
 
     def step(j, carry):
         i = heads - 1 - j
         h = flip(i)
-        parts[h] = column_part(h, 1 - member)
+        column_parts(h)
         swap(h).start()
 
         @pl.when(j > 0)
         def _():
             hand_over(i + 1)
-        grads[h] = column_part(h, member) + u_rows[h, :SW, :]
         return carry
 
     lax.fori_loop(0, heads, step, 0)
@@ -537,6 +549,8 @@
     encode(head)
     own_code = pltpu.make_async_copy(code_out.at[head], code_in.at[head], own_sem.at[1])
     own_code.start()
+    own_peak = pltpu.make_async_copy(peak_out.at[head], peak_in.at[head], own_sem.at[2])
+    own_peak.start()
     for i in range(1, head_shards):
         peer = lax.rem(shard + i, head_shards)
         remote(sums.at[peer], sums.at[peer], s_send.at[0], s_recv.at[peer], {"head": peer}).wait_recv()
@@ -550,46 +564,42 @@
         swap(flip(i)).wait_send()
     for i in range(1, heads):
         give(i, flip(i)).wait_send()
+        give_peak(i, flip(i)).wait_send()
     own_code.wait()
+    own_peak.wait()
     for i in range(1, heads):
         h = flip(i)
         remote(code_out.at[h], code_in.at[h], g_send.at[0], g_recv.at[h], mate).wait_recv()
-
-def decode_kernel(heads, codes, loss_in, grad_out, loss_out, flat, tall, sem):
+        remote(peak_out.at[h], peak_in.at[h], k_send.at[0], k_recv.at[h], mate).wait_recv()
+
+def decode_kernel(heads, codes, peaks, loss_in, grad_out, loss_out, flat):
     loss_out[0, 0] = loss_in[0, 0]
-    chunks = heads * SW // LANES
-
-    def write(c):
-        columns = pl.ds(c * LANES, LANES)
-        return pltpu.make_async_copy(tall.at[:, columns], grad_out.at[:, columns], sem.at[c])
-
     ready = 0
     for h in range(heads):
         code = codes[h].astype(jnp.float32)
-        flat[h * SW:(h + 1) * SW, :] = jnp.log(code[:SW]) * (code[SW:SW + 1] * (LOG2E / SPAN))
+        flat[h * SW:(h + 1) * SW, :] = jnp.log(code) * (peaks[h] * (LOG2E / SPAN))
         while (ready + 1) * LANES <= (h + 1) * SW:
-            tall[:, ready * LANES:(ready + 1) * LANES] = flat[ready * LANES:(ready + 1) * LANES, :].T
-            write(ready).start()
+            columns = slice(ready * LANES, (ready + 1) * LANES)
+            grad_out[:, columns] = flat[columns, :].T
             ready += 1
-    for c in range(chunks):
-        write(c).wait()
 
 
 def decode_call(heads, block):
     smem = pl.BlockSpec(memory_space=pltpu.SMEM)
     return pl.pallas_call(
         functools.partial(decode_kernel, heads),
+        grid=(block // LANES,),
         out_shape=(
             jax.ShapeDtypeStruct((block, heads * SW), jnp.float32),
             jax.ShapeDtypeStruct((1, 1), jnp.float32),
         ),
-        in_specs=[pl.BlockSpec(memory_space=pltpu.VMEM), smem],
-        out_specs=(pl.BlockSpec(memory_space=pl.ANY), smem),
-        scratch_shapes=[
-            pltpu.VMEM((heads * SW, block), jnp.float32),
-            pltpu.VMEM((block, heads * SW), jnp.float32),
-            pltpu.SemaphoreType.DMA((heads * SW // LANES,)),
+        in_specs=[
+            pl.BlockSpec((heads, SW, LANES), lambda i: (0, 0, i)),
+            pl.BlockSpec((heads, 1, LANES), lambda i: (0, 0, i)),
+            smem,
         ],
+        out_specs=(pl.BlockSpec((LANES, heads * SW), lambda i: (i, 0)), smem),
+        scratch_shapes=[pltpu.VMEM((heads * SW, LANES), jnp.float32)],
     )
 
 
@@ -600,11 +610,14 @@
     return pl.pallas_call(
         functools.partial(pair_kernel, heads, head_shards),
         out_shape=(
-            jax.ShapeDtypeStruct((heads, LANES, block), bf16),
+            jax.ShapeDtypeStruct((heads, SW, block), bf16),
+            jax.ShapeDtypeStruct((heads, 1, block), f32),
             jax.ShapeDtypeStruct((1, 1), f32),
         ),
         in_specs=[pl.BlockSpec(memory_space=pl.ANY), vmem, vmem],
-        out_specs=(pl.BlockSpec(memory_space=pl.ANY), pl.BlockSpec(memory_space=pltpu.SMEM)),
+        out_specs=(
+            pl.BlockSpec(memory_space=pl.ANY), pl.BlockSpec(memory_space=pl.ANY), pl.BlockSpec(memory_space=pltpu.SMEM)
+        ),
         scratch_shapes=[
             pltpu.VMEM((heads * SW, block), bf16),
             pltpu.VMEM((8, block), f32),
@@ -623,10 +636,10 @@
             pltpu.VMEM((heads, 8, block), f32),
             pltpu.VMEM((heads, LANES, block), f32),
             pltpu.VMEM((heads, LANES, block), f32),
+            pltpu.VMEM((heads, 2, SW, block), f32),
             pltpu.VMEM((heads, SW, block), f32),
-            pltpu.VMEM((heads, SW, block), f32),
-            pltpu.VMEM((heads, SW, block), f32),
-            pltpu.VMEM((heads, LANES, block), bf16),
+            pltpu.VMEM((heads, SW, block), bf16),
+            pltpu.VMEM((heads, 1, block), f32),
             pltpu.VMEM((n, 8, LANES), f32),
             pltpu.VMEM((head_shards, 8, LANES), f32),
             dma((heads,)), dma((heads,)), dma((heads,)),
@@ -634,7 +647,8 @@
             dma((n,)), dma((n,)), dma((heads,)),
             dma((heads,)), dma((heads,)),
             dma((heads,)), dma((heads,)),
-            dma((n,)), dma((n,)), dma((head_shards,)), dma((head_shards,)), dma((2,)),
+            dma((n,)), dma((n,)), dma((head_shards,)), dma((head_shards,)), dma((3,)),
+            dma((heads,)), dma((heads,)),
         ],
         compiler_params=pltpu.CompilerParams(
             collective_id=1, has_side_effects=True, vmem_limit_bytes=60 * 2**20
@@ -650,9 +664,9 @@
     head_shards = lax.axis_size("head")
     assert n % heads == 0
     group = n // heads
-    if group == 2 and heads & (heads - 1) == 0 and heads * SW % LANES == 0 and n * n * block * block <= 2**24:
-        codes, loss = pair_call(heads, n, head_shards, block)(teacher[0], student[0], weights[None, :])
-        student_grad, loss = decode_call(heads, block)(codes, loss)
+    if group == 2 and heads & (heads - 1) == 0 and heads * SW % LANES == 0 and block % LANES == 0 and n * n * block * block <= 2**24:
+        codes, peaks, loss = pair_call(heads, n, head_shards, block)(teacher[0], student[0], weights[None, :])
+        student_grad, loss = decode_call(heads, block)(codes, peaks, loss)
         return (loss.reshape(()), student_grad[None])
     vmem = pl.BlockSpec(memory_space=pltpu.VMEM)
     dma = pltpu.SemaphoreType.DMA

time: 72 us -> 69.6 us (0.967)
  Pallas kernels: 71.2 us -> 68.8 us
    pallas_call x1, Pallas kernels: 67.9 us -> 66 us  [local(): pair_call(heads, n, head_shards, block)]
where the time goes in v3:
time: 69.6 us; the launch traced here: 69.5 us
  Pallas kernels  68.8 us (99%)
    pallas_call x1, Pallas kernels, local(): pair_call(heads, n, head_shards, block)  66 us
    pallas_call x1, Pallas kernels, local(): student_grad, loss = decode_call(heads, block)(codes, peaks, loss)  2.79 us

profile of v3, /device:TPU:0, one launch (start us, length us, event | category | flops | bytes accessed | tf_op | source)
XLA Modules:
  0.0 69.5 jit_solution(2479259540441130290)
XLA Ops:
  0.6 66.0 %shard_map.50 = (bf16[8,112,256]{2,1,0:T(8,128)(2,1)}, f32[8,1,256]{2,1,0:T(1,128)}, f32[1,1]{1,0:T(1,128)}) custom-call(bf16[256,2048]{1,0:T(8,128)(2,1)} %bitcast.5, bf16[256,896]{1,0:T(8,128)(2,1)} %bitcast.6, f32[1,256]{1,0:T(1,128)} %bitcast.7), custom_call_target="tpu_custom_call" | custom-call | tf_op jit(solution)/shard_map/pallas_call | solution.py:668
  66.7 2.8 %shard_map.51 = (f32[256,896]{1,0:T(8,128)}, f32[1,1]{1,0:T(1,128)}) custom-call(bf16[8,112,256]{2,1,0:T(8,128)(2,1)} %get-tuple-element.7.codes, f32[8,1,256]{2,1,0:T(1,128)} %get-tuple-element.8.peaks, f32[1,1]{1,0:T(1,128)} %get-tuple-element.9.loss_in), custom_call_target="tpu_custom_call" | custom-call | tf_op jit(solution)/shard_map/pallas_call | solution.py:669

commit v4 on v3

--- a/solution.py
+++ b/solution.py
@@ -274,7 +274,7 @@
 
 def pair_kernel(
     heads, head_shards, t_in, s_in, w_in, code_in, peak_in, loss_out,
-    u_in, w_tile, t_all, u_all, u_turn, w_all, t_raw, u_raw, t_exp, u_exp, t_refs, u_refs, t_top, u_top, cross,
+    u_in, t_all, u_all, u_turn, w_all, t_raw, u_raw, t_exp, u_exp, t_refs, u_refs, t_top, u_top, cross,
     t_rows, u_rows, parts, landed_parts, code_out, peak_out, losses, sums,
     t_send, u_send, w_send, t_fwd, u_fwd, t_recv, u_recv, w_recv, p_send, p_recv, g_send, g_recv,
     l_send, l_recv, s_send, s_recv, own_sem, k_send, k_recv,
@@ -336,7 +336,6 @@
     ones = jnp.where(spare == 0, 1.0, 0.0).astype(jnp.bfloat16)
     for k in range(n):
         u_turn[k, SW:, :] = ones
-    w_tile[...] = jnp.broadcast_to(w_in[...], w_tile.shape)
     pl.semaphore_wait(barrier, n + head_shards - 2)
 
     direct = []
@@ -346,7 +345,7 @@
         direct += [
             remote(t_in.at[:, columns(h)], t_all.at[rows(me)], t_send.at[i], t_recv.at[me], device),
             remote(u_in.at[head_rows(h)], u_turn.at[me, pl.ds(0, SW)], u_send.at[i], u_recv.at[me], device),
-            remote(w_tile, w_all.at[head], w_send.at[i], w_recv.at[head], device),
+            remote(w_in, w_all.at[head], w_send.at[i], w_recv.at[head], device),
         ]
     for copy in direct:
         copy.start()
@@ -366,7 +365,7 @@
     own_t = pltpu.make_async_copy(t_in.at[:, columns(head)], t_all.at[rows(me)], own_sem.at[0])
     own_t.start()
     u_turn[me, :SW, :] = u_in[head_rows(head), :]
-    w_all[head] = w_tile[...]
+    w_all[head] = w_in[...]
     lane = lax.broadcasted_iota(jnp.int32, (block, LANES), 1)
 
     def turn_u(slot):
@@ -458,7 +457,7 @@
 
     lax.fori_loop(1, heads, arrival, 0)
     for i in range(1, heads):
-        remote(w_tile, w_all.at[flip(i)], w_send.at[0], w_recv.at[flip(i)], mate).wait_recv()
+        remote(w_in, w_all.at[flip(i)], w_send.at[0], w_recv.at[flip(i)], mate).wait_recv()
 
     loss = jnp.zeros((1, block), jnp.float32)
     for h in range(heads):
@@ -620,11 +619,10 @@
         ),
         scratch_shapes=[
             pltpu.VMEM((heads * SW, block), bf16),
-            pltpu.VMEM((8, block), f32),
             pltpu.VMEM((n * block, TW), bf16),
             pltpu.VMEM((n * block, LANES), bf16),
             pltpu.VMEM((n, LANES, block), bf16),
-            pltpu.VMEM((heads, 8, block), f32),
+            pltpu.VMEM((heads, 1, block), f32),
             pltpu.VMEM((2, 2 * block, block), f32),
             pltpu.VMEM((2, 2 * block, block), f32),
             pltpu.VMEM((heads, n, block, block), bf16),

time: 69.6 us -> 68.2 us (0.980)
  Pallas kernels: 68.8 us -> 67.3 us
    pallas_call x1, Pallas kernels: 66 us -> 64.5 us  [local(): pair_call(heads, n, head_shards, block)]
where the time goes in v4:
time: 68.2 us; the launch traced here: 68 us
  Pallas kernels  67.3 us (99%)
    pallas_call x1, Pallas kernels, local(): pair_call(heads, n, head_shards, block)  64.5 us
    pallas_call x1, Pallas kernels, local(): student_grad, loss = decode_call(heads, block)(codes, peaks, loss)  2.79 us

profile of v4, /device:TPU:0, one launch (start us, length us, event | category | flops | bytes accessed | tf_op | source)
XLA Modules:
  0.0 68.0 jit_solution(6698201383735592860)
XLA Ops:
  0.6 64.5 %shard_map.50 = (bf16[8,112,256]{2,1,0:T(8,128)(2,1)}, f32[8,1,256]{2,1,0:T(1,128)}, f32[1,1]{1,0:T(1,128)}) custom-call(bf16[256,2048]{1,0:T(8,128)(2,1)} %bitcast.5, bf16[256,896]{1,0:T(8,128)(2,1)} %bitcast.6, f32[1,256]{1,0:T(1,128)} %bitcast.7), custom_call_target="tpu_custom_call" | custom-call | tf_op jit(solution)/shard_map/pallas_call | solution.py:666
  65.2 2.8 %shard_map.51 = (f32[256,896]{1,0:T(8,128)}, f32[1,1]{1,0:T(1,128)}) custom-call(bf16[8,112,256]{2,1,0:T(8,128)(2,1)} %get-tuple-element.7.codes, f32[8,1,256]{2,1,0:T(1,128)} %get-tuple-element.8.peaks, f32[1,1]{1,0:T(1,128)} %get-tuple-element.9.loss_in), custom_call_target="tpu_custom_call" | custom-call | tf_op jit(solution)/shard_map/pallas_call | solution.py:667
